TPU v7x, 32 devices: a whole 2x2x4 slice. The times are simulated.
32 devices in a mesh: scene: 2 (over x), az: 16 (over z, y, core).
Axes of the slice: x: 2, y: 2, z: 4, core: 2. Of those that a mesh axis runs over, the one named last changes fastest.
Arguments:
- secondary: bfloat16 [2, 512, 12288], P(None, ('scene', 'az')), parts along dimension 1, may hold values from -6 to 6
- line_valid: int32 [512], P(('scene', 'az')), parts along dimension 0, may hold values 0 or 1
- first_valid: int32 [512], P(('scene', 'az')), parts along dimension 0, may hold values from 0 to 3071
- last_valid: int32 [512], P(('scene', 'az')), parts along dimension 0, may hold values from 9216 to 12288
- az_coef: float32 [3, 512], P(None, ('scene', 'az')), parts along dimension 1, may hold values from -0.33 to 0.33
- az_base: int32 [512], P(('scene', 'az')), parts along dimension 0, may hold values from -3 to 3
- rg_base: int32 [512], P(('scene', 'az')), parts along dimension 0, may hold values from -8 to 8
- rg_coef: float32 [8], P('scene'), parts along dimension 0, may hold values from -3 to 3
- block_dest: int32 [512], P(('scene', 'az')), parts along dimension 0, may hold values from 0 to 255, as said below
Outputs:
- coreg: bfloat16 [2, 512, 12288], P(None, ('scene', 'az')), parts along dimension 1
- mean_power: float32 [2], P('scene'), parts along dimension 0
- valid_share: float32 [2], P('scene'), parts along dimension 0
There are 2 independent parts, one for each index of `scene`. A program takes and returns all parts, laid end to end along the dimension named above; each array names one. Nothing has to cross between parts.
Inputs may be any that keep to these rules, and one draw needn't show every extreme that they name: `block_dest`: A permutation of 0 to 255. The 16 line blocks of each device of az take exactly one place on every device of az, itself included (place // 16 runs over all devices).
All inputs are finite; a program needn't handle non-finite values. No bound on the sum of `line_valid` on one device may be relied on, other than what follows from the above.
Results may differ from a plain program's by a relative error of at most 0.0066.
Values may be sent and summed in bfloat16 or wider, within the bound.
A program may use at most 128 MiB of HBM per device.

v0:
```python
import jax
import jax.numpy as jnp
from jax import lax
from jax.sharding import PartitionSpec as P

LINES = 1
RBMAX = 8
HALO = 7


def with_halo(block, sides, width):
    for axis, dim in sides:
        count = lax.axis_size(axis)
        forward = [(i, i + 1) for i in range(count - 1)]
        backward = [(target, source) for source, target in forward]
        low = lax.ppermute(
            lax.slice_in_dim(block, block.shape[dim] - width, None, axis=dim), axis, forward
        )
        high = lax.ppermute(lax.slice_in_dim(block, 0, width, axis=dim), axis, backward)
        block = jnp.concatenate([low, block, high], axis=dim)
    return block


def sinc_taper(distance):
    in_reach = jnp.abs(distance) < 4.0
    shaped = jnp.sinc(distance) * (0.5 + 0.5 * jnp.cos(jnp.pi * distance / 4.0))
    return jnp.where(in_reach, shaped, jnp.zeros_like(distance))


def tap_weights(az_coef, line_count):
    position = (jnp.arange(line_count, dtype=jnp.float32) + 0.5) / line_count
    fraction = (
        az_coef[0][:, None]
        + az_coef[1][:, None] * position
        + az_coef[2][:, None] * position * position
    )
    tap_offsets = jnp.arange(9, dtype=jnp.float32) - 4.0
    return sinc_taper(tap_offsets[None, None, :] - fraction[:, :, None]).astype(jnp.bfloat16)


def range_tiles(rg_coef, col_count):
    tile_total = col_count // 128
    col_index = jnp.arange(col_count, dtype=jnp.float32)
    along = (col_index + 0.5) / col_count
    offsets = (
        rg_coef[0]
        + rg_coef[1] * along
        + rg_coef[2] * along * along
        + rg_coef[3] * along * along * along
    )
    offsets = offsets.reshape(tile_total, 128)
    inner = jnp.arange(128, dtype=jnp.float32)
    tile_gaps = (jnp.arange(3, dtype=jnp.float32) - 1.0) * 128.0
    distance = (
        tile_gaps[:, None, None, None]
        + inner[None, None, :, None]
        - inner[None, None, None, :]
        - offsets[None, :, None, :]
    )
    return sinc_taper(distance).astype(jnp.bfloat16)


def range_apply(lines, kernel):
    col_count = lines.shape[-1]
    tile_total = col_count // 128
    tiled_rows = lines.reshape(lines.shape[:-1] + (tile_total, 128))
    padded = jnp.pad(tiled_rows, ((0, 0), (0, 0), (1, 1), (0, 0)))
    ranged = jnp.zeros(tiled_rows.shape, jnp.float32)
    for shift_tile in range(3):
        ranged = ranged + jnp.einsum(
            "npti,tij->nptj",
            padded[:, :, shift_tile : shift_tile + tile_total],
            kernel[shift_tile],
            preferred_element_type=jnp.float32,
        )
    return ranged.reshape(lines.shape).astype(jnp.bfloat16)


def shards(
    secondary, line_valid, first_valid, last_valid, az_coef, az_base, rg_base, rg_coef, block_dest
):
    col_count = secondary.shape[2]
    blocks = block_dest.shape[0]
    row_total = blocks * LINES
    col_index = jnp.arange(col_count, dtype=jnp.int32)
    kept_mask = (
        (line_valid[:, None] > 0)
        & (col_index[None, :] >= first_valid[:, None])
        & (col_index[None, :] < last_valid[:, None])
    )
    masked = jnp.where(kept_mask[None], secondary, jnp.zeros((), jnp.bfloat16))
    own_count = jnp.sum(kept_mask.astype(jnp.int32)).astype(jnp.float32)
    extended = with_halo(masked, (("az", 1),), HALO)
    padded = jnp.pad(extended, ((0, 0), (0, 0), (RBMAX, RBMAX)))
    span = row_total + 2 * HALO
    weights = tap_weights(az_coef, LINES)
    kernel = range_tiles(rg_coef, col_count)
    target = block_dest // blocks
    places = block_dest % blocks
    send_order = jnp.zeros((blocks,), jnp.int32).at[target].set(jnp.arange(blocks, dtype=jnp.int32))
    line_pos = (
        jnp.arange(blocks, dtype=jnp.int32)[:, None] * LINES
        + jnp.arange(LINES, dtype=jnp.int32)[None, :]
        + az_base[:, None]
        - 4
        + HALO
    )
    source_lines = jnp.arange(span, dtype=jnp.int32)
    taps = jnp.arange(9, dtype=jnp.int32)
    hit = (
        source_lines[None, None, None, :] == line_pos[:, :, None, None] + taps[None, None, :, None]
    )
    band = jnp.sum(jnp.where(hit, weights[..., None].astype(jnp.float32), 0.0), axis=2)
    band = band[send_order]
    shift_sent = rg_base[send_order]
    summed = jnp.zeros((row_total, 2, col_count), jnp.float32)
    for shift in range(-RBMAX, RBMAX + 1):
        picked = (
            jnp.where((shift_sent == shift)[:, None, None], band, 0.0)
            .astype(jnp.bfloat16)
            .reshape(row_total, span)
        )
        summed = summed + jnp.einsum(
            "rs,psc->rpc",
            picked,
            padded[:, :, RBMAX + shift : RBMAX + shift + col_count],
            preferred_element_type=jnp.float32,
        )
    azimuthal = summed.astype(jnp.bfloat16)
    sent_places = places[send_order]
    tag_grid = sent_places[:, None]
    line_part = lax.all_to_all(
        azimuthal.reshape(blocks, LINES, 2, col_count),
        "az",
        split_axis=0,
        concat_axis=0,
        tiled=True,
    )
    tag_part = lax.all_to_all(tag_grid, "az", split_axis=0, concat_axis=0, tiled=True)
    done = range_apply(line_part.reshape((-1,) + line_part.shape[2:]), kernel)
    arrived = done.reshape(line_part.shape)
    place_tags = tag_part[:, 0]
    own_power = jnp.sum(jnp.square(arrived.astype(jnp.float32)))
    total_power, total_count = lax.psum((own_power, own_count), "az")
    mean_power = total_power / jnp.maximum(total_count, 1.0)
    power_gain = lax.rsqrt(mean_power + 0.5)
    arrange = (place_tags[None, :] == jnp.arange(blocks, dtype=jnp.int32)[:, None]).astype(
        jnp.bfloat16
    )
    ordered = jnp.einsum("qb,blpc->pqlc", arrange, arrived, preferred_element_type=jnp.float32)
    scaled = (ordered * power_gain).astype(jnp.bfloat16)
    coregistered = scaled.reshape(2, row_total, col_count)
    valid_share = total_count / float(col_count * row_total * lax.axis_size("az"))
    return (coregistered, mean_power.reshape(1), valid_share.reshape(1))


def solution(mesh):
    placed = (
        P(None, ("scene", "az"), None),
        P(("scene", "az")),
        P(("scene", "az")),
        P(("scene", "az")),
        P(None, ("scene", "az")),
        P(("scene", "az")),
        P(("scene", "az")),
        P("scene"),
        P(("scene", "az")),
    )
    return jax.shard_map(
        shards,
        mesh=mesh,
        in_specs=placed,
        out_specs=(P(None, ("scene", "az"), None), P("scene"), P("scene")),
        check_vma=False,
    )
```

profile of v0, /device:TPU:0, one launch (start us, length us, event | category | flops | bytes accessed | tf_op | source)
XLA Modules:
  0.0 184.3 jit_solution(3026352699120998335)
XLA Ops:
  0.6 0.7 and_select_fusion
  2.6 0.7 copy.31
  3.3 7.4 %all-to-all-start.1 = ((s32[16,1,1]{2,1,0:T(1,128)}), s32[16,1,1]{2,1,0:T(1,128)S(1)}, u32[]{:S(2)}, u32[]{:S(2)}) async-start(s32[16,1,1]{2,1,0:T(1,128)} %copy.31), calls=%async_computation.1 | async-start | bytes 16384 | tf_op jit(solution)/shard_map/all_to_all | solution.py:139
  10.7 0.7 broadcast_compare_fusion.17
  11.4 1.0 fusion.61
  12.4 1.2 broadcast_select_fusion
  13.7 2.3 %collective-permute-start = (bf16[2,7,12288]{2,1,0:T(8,128)(2,1)S(1)}, bf16[2,7,12288]{2,1,0:T(8,128)(2,1)S(1)}, u32[]{:S(2)}, u32[]{:S(2)}) collective-permute-start(bf16[2,7,12288]{2,1,0:T(8,128)(2,1)S(1)} %get-tuple-element.5), channel_id=1, source_target_pairs={{0,1},{1,2},{2,3},{3,4},{4,5},{5,6},{6,7},{7,8},{8,9},{9,10},{10,1... | collective-permute-start | bytes 1032200 | tf_op jit(solution)/shard_map/ppermute | solution.py:16
  16.1 1.3 collective-permute-start.1
  21.6 0.7 fusion.64
  24.2 0.7 convolution_add_fusion.14
  28.9 0.8 fusion.30
  30.9 0.7 convolution_add_fusion.4
  31.6 0.7 convolution_add_fusion.3
  32.2 0.7 convolution_add_fusion.2
  33.6 0.7 fusion.34
  34.2 1.9 %copy.26 = bf16[16,1,2,12288]{3,2,1,0:T(2,128)(2,1)} copy(bf16[16,1,2,12288]{3,0,2,1:T(8,128)(2,1)S(1)} %fusion.34) | data formatting | bytes 1572864 | tf_op jit(solution)/shard_map/reshape | solution.py:133
  36.1 10.0 %all-to-all-start = ((bf16[16,1,2,12288]{3,2,1,0:T(2,128)(2,1)}), bf16[16,1,2,12288]{3,2,1,0:T(2,128)(2,1)S(1)}, u32[]{:S(2)}, u32[]{:S(2)}) async-start(bf16[16,1,2,12288]{3,2,1,0:T(2,128)(2,1)} %copy.26), calls=%async_computation | async-start | bytes 1572864 | tf_op jit(solution)/shard_map/all_to_all | solution.py:132
  46.2 86.0 %fusion.29 = bf16[3,96,128,128]{3,2,1,0:T(8,128)(2,1)} fusion(f32[96,128]{1,0:T(8,128)S(1)} %fusion.64, f32[3,128,128]{2,1,0:T(8,128)S(1)} %iota_subtract_fusion), kind=kLoop, calls=%fused_computation.41 | loop fusion | flops 193462272 | bytes 9682944 | tf_op jit(solution)/shard_map/convert_element_type | solution.py:60
  132.2 0.9 convert_reduce_fusion
  135.2 2.9 %fusion.36 = f32[96,128,16,2]{1,2,3,0:T(8,128)S(1)} fusion(bf16[3,96,128,128]{3,2,1,0:T(8,128)(2,1)} %fusion.29, bf16[16,2,96,128]{3,2,1,0:T(8,128)(2,1)S(1)} %reshape.688), kind=kOutput, calls=%fused_computation.66 | convolution fusion | flops 100663296 | bytes 5505024 | tf_op jit(solution)/shard_map/npti,tij->nptj/dot_general | solution.py:70
  138.1 2.8 %fusion.35 = f32[96,128,16,2]{1,2,3,0:T(8,128)S(1)} fusion(bf16[3,96,128,128]{3,2,1,0:T(8,128)(2,1)} %fusion.29, bf16[16,2,96,128]{3,0,1,2:T(8,128)(2,1)S(1)} %copy.28), kind=kOutput, calls=%fused_computation.64 | convolution fusion | flops 100663296 | bytes 5505024 | tf_op jit(solution)/shard_map/npti,tij->nptj/dot_general | solution.py:70
  140.9 3.4 %multiply_reduce_fusion = (f32[]{:T(128)}, bf16[96,128,16,2]{1,2,3,0:T(8,128)(2,1)S(1)}) fusion(f32[96,128,16,2]{1,2,3,0:T(8,128)S(1)} %fusion.35, f32[96,128,16,2]{1,2,3,0:T(8,128)S(1)} %fusion.36, bf16[16,2,96,128]{3,0,1,2:T(8,128)(2,1)S(1)} %copy.28, bf16[3,96,128,128]{3,2,1,0:T(8,128)(2,1)} %fusion.29), kind=kOutput, calls=%fused_computation.70 | convolution fusion | flops 103022592 | bytes 7864324 | tf_op jit(solution)/shard_map/npti,tij->nptj/dot_general | solution.py:70
  144.4 34.4 %all-reduce.2 = (f32[]{:T(128)}, f32[]{:T(128)}) all-reduce(f32[]{:T(128)} %get-tuple-element.30, f32[]{:T(128)S(6)} %convert_element_type.203), channel_id=1, replica_groups=mesh['scene'=2,'az'=16] {'az'}, use_global_device_ids=true, to_apply=%region_3.4 | all-reduce | flops 2 | bytes 16 | tf_op jit(solution)/shard_map/psum | solution.py:144
  180.8 1.2 fusion.33
  (50 shorter events, 12.9 us)
Async XLA Ops:
  0.6 16.9 %copy-start = (s32[16]{0:T(128)S(1)}, s32[16]{0:T(128)}, u32[]{:S(2)}) copy-start(s32[16]{0:T(128)} %param.15) | copy-start | bytes 196
  3.3 32.8 %all-to-all-start.1 = ((s32[16,1,1]{2,1,0:T(1,128)}), s32[16,1,1]{2,1,0:T(1,128)S(1)}, u32[]{:S(2)}, u32[]{:S(2)}) async-start(s32[16,1,1]{2,1,0:T(1,128)} %copy.31), calls=%async_computation.1 | async-start | bytes 16384 | tf_op jit(solution)/shard_map/all_to_all | solution.py:139
  12.4 5.1 %copy-start.2 = (f32[3,16]{1,0:T(4,128)S(1)}, f32[3,16]{1,0:T(4,128)}, u32[]{:S(2)}) copy-start(f32[3,16]{1,0:T(4,128)} %param.13) | copy-start | bytes 580
  12.4 5.1 %copy-start.5 = (s32[16]{0:T(128)S(1)}, s32[16]{0:T(128)}, u32[]{:S(2)}) copy-start(s32[16]{0:T(128)} %param.14) | copy-start | bytes 196
  12.4 6.1 %copy-start.1 = (f32[4]{0:T(128)S(1)}, f32[4]{0:T(128)}, u32[]{:S(2)}) copy-start(f32[4]{0:T(128)} %param.16) | copy-start | bytes 52
  13.7 8.7 %collective-permute-start = (bf16[2,7,12288]{2,1,0:T(8,128)(2,1)S(1)}, bf16[2,7,12288]{2,1,0:T(8,128)(2,1)S(1)}, u32[]{:S(2)}, u32[]{:S(2)}) collective-permute-start(bf16[2,7,12288]{2,1,0:T(8,128)(2,1)S(1)} %get-tuple-element.5), channel_id=1, source_target_pairs={{0,1},{1,2},{2,3},{3,4},{4,5},{5,6},{6,7},{7,8},{8,9},{9,10},{10,1... | collective-permute-start | bytes 1032200 | tf_op jit(solution)/shard_map/ppermute | solution.py:16
  16.1 6.4 %collective-permute-start.1 = (bf16[2,7,12288]{2,1,0:T(8,128)(2,1)S(1)}, bf16[2,7,12288]{2,1,0:T(8,128)(2,1)S(1)}, u32[]{:S(2)}, u32[]{:S(2)}) collective-permute-start(bf16[2,7,12288]{2,1,0:T(8,128)(2,1)S(1)} %get-tuple-element.6), channel_id=1, source_target_pairs={{1,0},{2,1},{3,2},{4,3},{5,4},{6,5},{7,6},{8,7},{9,8},{10,9},{11,1... | collective-permute-start | bytes 1032200 | tf_op jit(solution)/shard_map/ppermute | solution.py:19
  36.1 98.0 %all-to-all-start = ((bf16[16,1,2,12288]{3,2,1,0:T(2,128)(2,1)}), bf16[16,1,2,12288]{3,2,1,0:T(2,128)(2,1)S(1)}, u32[]{:S(2)}, u32[]{:S(2)}) async-start(bf16[16,1,2,12288]{3,2,1,0:T(2,128)(2,1)} %copy.26), calls=%async_computation | async-start | bytes 1572864 | tf_op jit(solution)/shard_map/all_to_all | solution.py:132
  46.1 86.0 %copy-start.3 = (s32[16]{0:T(128)S(1)}, s32[16]{0:T(128)}, u32[]{:S(2)}) copy-start(s32[16]{0:T(128)} %param.12) | copy-start | bytes 196
  46.2 86.0 %copy-start.4 = (s32[16]{0:T(128)S(1)}, s32[16]{0:T(128)}, u32[]{:S(2)}) copy-start(s32[16]{0:T(128)} %param.11) | copy-start | bytes 196
where the time goes:
time: 185 us; the launch traced here: 184 us
  other arithmetic  92.5 us (50%)
  blocking collectives  34.4 us (19%)
  matrix products  21.6 us (12%)
  starting transfers between devices  21.1 us (11%)
  between operations  7.76 us (4%)
  local copies, waits for them, and re-layouts  6.95 us (4%)
    convert_element_type x1, other arithmetic, range_tiles(): return sinc_taper(distance).astype(jnp.bfloat16)  86 us
    psum x1, blocking collectives, shards(): total_power, total_count = lax.psum((own_power, own_count), 'az')  34.4 us
    dot_general x17, matrix products, shards(): jnp.einsum('rs,psc->rpc', picked, padded[:, :, RBMAX + shift:RBMAX + shif...  11.2 us
    all_to_all x1, starting transfers between devices, shards(): lax.all_to_all(azimuthal.reshape(blocks, LINES, 2, col_count), 'az', spli...  10 us
    dot_general x3, matrix products, range_apply(): jnp.einsum('npti,tij->nptj', padded[:, :, shift_tile:shift_tile + tile_to...  9.14 us
    all_to_all x1, starting transfers between devices, shards(): lax.all_to_all(tag_grid, 'az', split_axis=0, concat_axis=0, tiled=True)  7.41 us
  transfers between devices with their start and end apart: 4, of which 0 were waited for; matrix products, arithmetic and copies ran while one was open for 58% of the time, Pallas kernels for 0%

commit v1 on v0

v1 whole, which is shorter than its diff:
```python
import functools

import jax
import jax.numpy as jnp
from jax import lax
from jax.experimental import pallas as pl
from jax.experimental.pallas import tpu as pltpu
from jax.sharding import PartitionSpec as P

HALO = 8
TAPS = 11
PAD = 8
META = 16
PI = 3.141592653589793


def sinc_taper(distance):
    in_reach = jnp.abs(distance) < 4.0
    shaped = jnp.sinc(distance) * (0.5 + 0.5 * jnp.cos(jnp.pi * distance / 4.0))
    return jnp.where(in_reach, shaped, jnp.zeros_like(distance))


def azimuth_band(az_coef, az_base):
    blocks = az_base.shape[0]
    q = 0.5
    fraction = az_coef[0] + az_coef[1] * q + az_coef[2] * q * q
    held = jnp.arange(blocks + 2 * HALO, dtype=jnp.int32)
    own, low = held, held - blocks - HALO
    high = held - HALO
    row = jnp.where(held < blocks, own, jnp.where(held < blocks + HALO, low, high))
    gap = row[None, :] - jnp.arange(blocks, dtype=jnp.int32)[:, None] - az_base[:, None]
    value = sinc_taper(gap.astype(jnp.float32) - fraction[:, None])
    return jnp.where(jnp.abs(gap) <= 4, value, 0.0).astype(jnp.bfloat16)


def split3(x):
    hi = x.astype(jnp.bfloat16).astype(jnp.float32)
    rest = x - hi
    mid = rest.astype(jnp.bfloat16).astype(jnp.float32)
    return hi, mid, rest - mid


def filter_kernel(
    coef, shift, dest, valid, first, last, band, mid, low, high, sent, dense, weight, start
):
    blocks, cols = mid.shape[1], mid.shape[2]
    tiles = cols // 128
    groups = tiles // 8
    span = tiles + 2 * PAD

    for g in range(groups):
        centre = (g * 1024 + 512) / cols
        oc = coef[0] + coef[1] * centre + coef[2] * (centre * centre) + coef[3] * (centre**3)
        n0 = (oc - 5.0 + 64.0).astype(jnp.int32) - 63
        start[g] = n0
        sub = lax.broadcasted_iota(jnp.int32, (8, 128), 0)
        lane = lax.broadcasted_iota(jnp.int32, (8, 128), 1)
        col = g * 1024 + sub * 128 + lane
        v = (col.astype(jnp.float32) + 0.5) / cols
        off = coef[0] + coef[1] * v + coef[2] * v * v + coef[3] * v * v * v
        whole = jnp.round(off)
        part = off - whole
        odd = (whole.astype(jnp.int32) + n0) & 1
        sine = jnp.sin(PI * part) * (-1.0 / PI) * (1 - 2 * odd).astype(jnp.float32)
        base = (n0.astype(jnp.float32) - off) * (PI / 4.0)
        c0, s0 = jnp.cos(base), jnp.sin(base)
        for k in range(TAPS):
            n = n0 + k
            d = n.astype(jnp.float32) - off
            ck, sk = COS8[k % 8], COS8[(k - 2) % 8]
            taper = 0.5 + 0.5 * (c0 * ck - s0 * sk)
            top = sine if k % 2 == 0 else -sine
            near = d == 0.0
            val = jnp.where(near, 1.0, top / jnp.where(near, 1.0, d)) * taper
            keep = (jnp.abs(d) < 4.0) & (col + n >= 0) & (col + n < cols)
            val = jnp.where(keep, val, 0.0)
            weight[g, k] = val.astype(jnp.bfloat16).astype(jnp.float32)

    zero = jnp.zeros((PAD, 128), jnp.float32)

    def clear(r, carry):
        dense[pl.ds(pl.multiple_of(r * span, 8), PAD), :] = zero
        dense[pl.ds(pl.multiple_of(r * span + PAD + tiles, 8), PAD), :] = zero
        return carry

    lax.fori_loop(0, 2 * blocks, clear, 0)
    weights_az = band[...]
    for p in range(2):

        def azimuth(i, carry):
            at = pl.ds(pl.multiple_of(i * 512, 512), 512)
            rows = jnp.concatenate([mid[p, :, at], low[p, :, at], high[p, :, at]], axis=0)
            out = jnp.dot(weights_az, rows, preferred_element_type=jnp.float32)
            out = out.astype(jnp.bfloat16).astype(jnp.float32)
            for u in range(4):
                place = p * blocks * span + PAD + i * 4 + u
                dense[pl.ds(place, blocks, stride=span), :] = out[:, u * 128 : u * 128 + 128]
            return carry

        lax.fori_loop(0, tiles // 4, azimuth, 0)

    lane = lax.broadcasted_iota(jnp.int32, (8, 128), 1)

    def group(big, power):
        def line(j, power):
            to = dest[j] // blocks
            for p in range(2):
                halves = []
                for h in range(2):
                    g = big * 2 + h
                    b = shift[j] + start[g]
                    q = jnp.where(b < 0, 1, 0)
                    b = b + 128 * q
                    at = (p * blocks + j) * span + PAD + g * 8 - q
                    x0 = dense[pl.ds(at, 8), :]
                    x1 = dense[pl.ds(at + 1, 8), :]
                    x2 = dense[pl.ds(at + 2, 8), :]
                    under = lane < b
                    back = 128 - b
                    y0 = pltpu.roll(jnp.where(under, x1, x0), back, 1)
                    y1 = pltpu.roll(jnp.where(under, x2, x1), back, 1)
                    acc = weight[g, 0] * y0
                    for k in range(1, TAPS):
                        moved = pltpu.roll(jnp.where(lane < k, y1, y0), 128 - k, 1)
                        acc = acc + weight[g, k] * moved
                    halves.append(acc)
                done = jnp.concatenate(halves, axis=0).astype(jnp.bfloat16)
                sent[to, pl.ds(pl.multiple_of(p * tiles + big * 16, 16), 16), :] = done
                wide = done.astype(jnp.float32)
                power = power + wide * wide
            return power

        return lax.fori_loop(0, blocks, line, power, unroll=2)

    power = lax.fori_loop(0, tiles // 16, group, jnp.zeros((16, 128), jnp.float32))
    own_power = jnp.broadcast_to(jnp.sum(power, keepdims=True), (META, 128))
    count = jnp.int32(0)
    for j in range(blocks):
        have = jnp.minimum(last[j], cols) - jnp.maximum(first[j], 0)
        count = count + jnp.where(valid[j] > 0, jnp.maximum(have, 0), 0)
    own_count = jnp.full((META, 128), count, jnp.int32).astype(jnp.float32)
    row = lax.broadcasted_iota(jnp.int32, (META, 128), 0)
    meta = jnp.zeros((META, 128), jnp.float32)
    for i, piece in enumerate(split3(own_power) + split3(own_count)):
        meta = jnp.where(row == i + 1, piece, meta)
    for j in range(blocks):
        place = jnp.full((META, 128), dest[j] % blocks, jnp.int32).astype(jnp.float32)
        note = jnp.where(row == 0, place, meta).astype(jnp.bfloat16)
        sent[dest[j] // blocks, pl.ds(2 * tiles, META), :] = note


HALF = 0.7071067811865476
COS8 = (1.0, HALF, 0.0, -HALF, -1.0, -HALF, 0.0, HALF)


def finish_kernel(total, got, out, mean, share, wide):
    blocks, cols = out.shape[1], out.shape[2]
    tiles = cols // 128
    notes = [got[s, pl.ds(2 * tiles, META), :].astype(jnp.float32) for s in range(blocks)]
    both = functools.reduce(lambda a, b: a + b, notes)
    power = both[1:2] + both[2:3] + both[3:4]
    count = both[4:5] + both[5:6] + both[6:7]
    mean_power = power / jnp.maximum(count, 1.0)
    gain = lax.rsqrt(mean_power + 0.5)
    mean[0] = mean_power[0, 0]
    share[0] = (count / float(total))[0, 0]
    for s in range(blocks):
        place = notes[s][0, 0].astype(jnp.int32)
        for p in range(2):
            x = got[s, pl.ds(p * tiles, tiles), :].astype(jnp.float32) * gain
            wide[pl.ds(pl.multiple_of((p * blocks + place) * tiles, 8), tiles), :] = x

    def tile(t, carry):
        at = pl.ds(pl.multiple_of(t * 128, 128), 128)
        for p in range(2):
            x = wide[pl.ds(p * blocks * tiles + t, blocks, stride=tiles), :]
            out[p, :, at] = x.astype(jnp.bfloat16)
        return carry

    lax.fori_loop(0, tiles, tile, 0, unroll=8)


def shards(
    secondary, line_valid, first_valid, last_valid, az_coef, az_base, rg_base, rg_coef, block_dest
):
    cols = secondary.shape[2]
    blocks = block_dest.shape[0]
    tiles = cols // 128
    count = lax.axis_size("az")
    col = jnp.arange(cols, dtype=jnp.int32)
    kept = (
        (line_valid[:, None] > 0)
        & (col[None, :] >= first_valid[:, None])
        & (col[None, :] < last_valid[:, None])
    )
    masked = jnp.where(kept[None], secondary, jnp.zeros((), jnp.bfloat16))
    forward = [(i, i + 1) for i in range(count - 1)]
    backward = [(b, a) for a, b in forward]
    low = lax.ppermute(masked[:, blocks - HALO :], "az", forward)
    high = lax.ppermute(masked[:, :HALO], "az", backward)
    band = azimuth_band(az_coef, az_base)
    smem = pl.BlockSpec(memory_space=pltpu.SMEM)
    vmem = pl.BlockSpec(memory_space=pltpu.VMEM)
    sent = pl.pallas_call(
        filter_kernel,
        out_shape=jax.ShapeDtypeStruct((blocks, 2 * tiles + META, 128), jnp.bfloat16),
        in_specs=[smem] * 6 + [vmem] * 4,
        out_specs=vmem,
        scratch_shapes=[
            pltpu.VMEM((2 * blocks * (tiles + 2 * PAD), 128), jnp.float32),
            pltpu.VMEM((tiles // 8, TAPS, 8, 128), jnp.float32),
            pltpu.SMEM((tiles // 8,), jnp.int32),
        ],
        cost_estimate=pl.CostEstimate(
            flops=40 * 2 * blocks * cols, bytes_accessed=8 * blocks * cols, transcendentals=0
        ),
        name="filters",
    )(rg_coef, rg_base, block_dest, line_valid, first_valid, last_valid, band, masked, low, high)
    got = lax.all_to_all(sent, "az", split_axis=0, concat_axis=0, tiled=True)
    return pl.pallas_call(
        functools.partial(finish_kernel, cols * blocks * count),
        out_shape=(
            jax.ShapeDtypeStruct((2, blocks, cols), jnp.bfloat16),
            jax.ShapeDtypeStruct((1,), jnp.float32),
            jax.ShapeDtypeStruct((1,), jnp.float32),
        ),
        in_specs=[vmem],
        out_specs=(vmem, smem, smem),
        scratch_shapes=[pltpu.VMEM((2 * blocks * tiles, 128), jnp.float32)],
        name="finish",
    )(got)


def solution(mesh):
    rows = P(("scene", "az"))
    placed = (
        P(None, ("scene", "az"), None),
        rows,
        rows,
        rows,
        P(None, ("scene", "az")),
        rows,
        rows,
        P("scene"),
        rows,
    )
    return jax.shard_map(
        shards,
        mesh=mesh,
        in_specs=placed,
        out_specs=(P(None, ("scene", "az"), None), P("scene"), P("scene")),
        check_vma=False,
    )
```

time: 185 us -> 71.8 us (0.39)
  other arithmetic: 92.5 us -> 2.91 us
  Pallas kernels: 0 us -> 24.3 us
  matrix products: 21.6 us -> 0 us
  starting transfers between devices: 21.1 us -> 4.47 us
  between operations: 7.76 us -> 0.72 us
  local copies, waits for them, and re-layouts: 6.95 us -> 3.03 us
    convert_element_type x2 -> x1, other arithmetic: 86.1 us -> 0.72 us  [azimuth_band(): return jnp.where(jnp.abs(gap) <= 4, value, 0.0).astype(jnp.bfloat16)]
    all_to_all x0 -> x1, blocking collectives: none -> 35.5 us  [shards(): got = lax.all_to_all(sent, 'az', split_axis=0, concat_axis=0, tiled=True)]
    psum x1 -> x0, blocking collectives: 34.4 us -> none  [shards(): total_power, total_count = lax.psum((own_power, own_count), 'az')]
    pallas_call x0 -> x2, Pallas kernels: none -> 24.3 us  [the longest x1 21 us: shards(): pl.pallas_call(filter_kernel, out_shape=jax.ShapeDtypeStruct((blocks, 2 *...]
    dot_general x21 -> x0, matrix products: 21.6 us -> none  [the longest x17 11.2 us: shards(): jnp.einsum('rs,psc->rpc', picked, padded[:, :, RBMAX + shift:RBMAX + shif...]
    all_to_all x2 -> x0, starting transfers between devices: 17.4 us -> none  [the longest x1 10 us: shards(): lax.all_to_all(azimuthal.reshape(blocks, LINES, 2, col_count), 'az', spli...]
    unnamed x12 -> x14, local copies, waits for them, and re-layouts: 0.04 us -> 2.97 us
    gather x3 -> x0, local copies, waits for them, and re-layouts: 1.89 us -> none  [the longest x1 0.66 us: shards(): sent_places = places[send_order]]
  transfers between devices with their start and end apart: 4 -> 2, of which waited for: 0 -> 0; matrix products, arithmetic and copies ran while one was open for 58% -> 1% of each run, Pallas kernels for 0% -> 0%
where the time goes in v1:
time: 71.8 us; the launch traced here: 70.9 us
  blocking collectives  35.5 us (49%)
  Pallas kernels  24.3 us (34%)
  starting transfers between devices  4.47 us (6%)
  local copies, waits for them, and re-layouts  3.03 us (4%)
  other arithmetic  2.91 us (4%)
  between operations  0.72 us (1%)
    all_to_all x1, blocking collectives, shards(): got = lax.all_to_all(sent, 'az', split_axis=0, concat_axis=0, tiled=True)  35.5 us
    pallas_call x1, Pallas kernels, shards(): pl.pallas_call(filter_kernel, out_shape=jax.ShapeDtypeStruct((blocks, 2 *...  21 us
    pallas_call x1, Pallas kernels, shards(): pl.pallas_call(functools.partial(finish_kernel, cols * blocks * count), o...  3.31 us
    ppermute x1, starting transfers between devices, shards(): low = lax.ppermute(masked[:, blocks - HALO:], 'az', forward)  3.05 us
    unnamed x14, local copies, waits for them, and re-layouts  2.97 us
  transfers between devices with their start and end apart: 2, of which 0 were waited for; matrix products, arithmetic and copies ran while one was open for 1% of the time, Pallas kernels for 0%

profile of v1, /device:TPU:0, one launch (start us, length us, event | category | flops | bytes accessed | tf_op | source)
XLA Modules:
  0.0 70.9 jit_solution(4142789947507789057)
XLA Ops:
  0.6 0.0 copy-start.4
  0.6 0.0 copy-start.3
  0.7 0.7 broadcast_compare_fusion
  1.3 0.0 copy-done.4
  1.3 0.0 copy-done.3
  1.3 0.3 fusion.1
  1.6 1.2 %broadcast_select_fusion.mid = bf16[2,16,12288]{2,1,0:T(8,128)(2,1)S(1)} fusion(bf16[2,16,12288]{2,1,0:T(8,128)(2,1)} %param.9, pred[16,12288]{1,0:T(8,128)(4,1)S(1)} %fusion.1), kind=kLoop, calls=%fused_computation.4 | loop fusion | flops 393216 | bytes 1769472 | tf_op jit(solution)/shard_map/jit(_where)/select_n | solution.py:196
  2.8 0.0 copy-start
  2.9 0.1 fusion.18
  2.9 0.8 %copy-done = bf16[2,16,12288]{2,1,0:T(8,128)(2,1)} copy-done((bf16[2,16,12288]{2,1,0:T(8,128)(2,1)}, bf16[2,16,12288]{2,1,0:T(8,128)(2,1)S(1)}, u32[]{:S(2)}) %copy-start) | copy-done | bytes 786456
  3.7 0.0 copy-start.5
  3.7 1.4 %collective-permute-start.1 = (bf16[2,8,12288]{2,1,0:T(8,128)(2,1)S(1)}, bf16[2,8,12288]{2,1,0:T(8,128)(2,1)S(1)}, u32[]{:S(2)}, u32[]{:S(2)}) collective-permute-start(bf16[2,8,12288]{2,1,0:T(8,128)(2,1)S(1)} %get-tuple-element.3), channel_id=1, source_target_pairs={{1,0},{2,1},{3,2},{4,3},{5,4},{6,5},{7,6},{8,7},{9,8},{10,9},{11,1... | collective-permute-start | bytes 1179656 | tf_op jit(solution)/shard_map/ppermute | solution.py:200
  5.2 3.1 %collective-permute-start = (bf16[2,8,12288]{2,1,0:T(8,128)(2,1)S(1)}, bf16[2,8,12288]{2,1,0:T(8,128)(2,1)S(1)}, u32[]{:S(2)}, u32[]{:S(2)}) collective-permute-start(bf16[2,8,12288]{2,1,0:T(8,128)(2,1)S(1)} %get-tuple-element.4), channel_id=1, source_target_pairs={{0,1},{1,2},{2,3},{3,4},{4,5},{5,6},{6,7},{7,8},{8,9},{9,10},{10,1... | collective-permute-start | bytes 1179656 | tf_op jit(solution)/shard_map/ppermute | solution.py:199
  8.2 0.0 copy-done.5
  8.2 0.0 copy-start.6
  8.3 0.6 copy-done.6
  8.9 0.7 %select_convert_fusion.band = bf16[16,32]{1,0:T(8,128)(2,1)} fusion(f32[16]{0:T(128)S(1)} %add_bitcast_fusion, s32[16]{0:T(128)S(1)} %copy-done.6, s32[32]{0:T(128)S(1)} %compare_select_fusion), kind=kLoop, calls=%fused_computation.19 | loop fusion | flops 24064 | bytes 1280 | tf_op jit(solution)/shard_map/convert_element_type | solution.py:33
  9.6 0.0 collective-permute-done.1.high
  9.6 0.0 collective-permute-done.low
  9.6 0.8 %copy-done.1 = bf16[2,8,12288]{2,1,0:T(8,128)(2,1)} copy-done((bf16[2,8,12288]{2,1,0:T(8,128)(2,1)}, bf16[2,8,12288]{2,1,0:T(8,128)(2,1)S(1)}, u32[]{:S(2)}) %copy-start.1) | copy-done | bytes 393240
  10.4 0.7 %copy-done.2 = bf16[2,8,12288]{2,1,0:T(8,128)(2,1)} copy-done((bf16[2,8,12288]{2,1,0:T(8,128)(2,1)}, bf16[2,8,12288]{2,1,0:T(8,128)(2,1)S(1)}, u32[]{:S(2)}) %copy-start.2) | copy-done | bytes 393240
  11.1 21.0 %filters.1 = bf16[16,208,128]{2,1,0:T(8,128)(2,1)} custom-call(f32[4]{0:T(128)} %coef.1, s32[16]{0:T(128)} %shift.1, s32[16]{0:T(128)} %dest.1, s32[16]{0:T(128)} %valid.1, s32[16]{0:T(128)} %first.1, s32[16]{0:T(128)} %last.1, bf16[16,32]{1,0:T(8,128)(2,1)} %select_convert_fusion.band, bf16[2,16,12288]{2,1,0:T(8,128)(2,1)} %copy-done, ...), custom_call_target="tpu_custom_call" | custom-call | flops 15728640 | bytes 1572864 | tf_op jit(solution)/shard_map/filters/pallas_call | solution.py:204
  32.1 35.5 %all_to_all.5.got = bf16[16,208,128]{2,1,0:T(8,128)(2,1)} all-to-all(bf16[16,208,128]{2,1,0:T(8,128)(2,1)} %filters.1), channel_id=1, replica_groups=mesh['scene'=2,'az'=16] {'az'}, dimensions={0} | all-to-all | bytes 1703936 | tf_op jit(solution)/shard_map/all_to_all | solution.py:219
  67.6 3.3 %finish.1 = (bf16[2,16,12288]{2,1,0:T(8,128)(2,1)}, f32[1]{0:T(128)}, f32[1]{0:T(128)}) custom-call(bf16[16,208,128]{2,1,0:T(8,128)(2,1)} %all_to_all.5.got), custom_call_target="tpu_custom_call" | custom-call | tf_op jit(solution)/shard_map/finish/pallas_call | solution.py:220
  (4 shorter events, 0.0 us)
Async XLA Ops:
  0.6 0.7 copy-start.4
  0.6 0.7 copy-start.3
  2.8 0.9 %copy-start = (bf16[2,16,12288]{2,1,0:T(8,128)(2,1)}, bf16[2,16,12288]{2,1,0:T(8,128)(2,1)S(1)}, u32[]{:S(2)}) copy-start(bf16[2,16,12288]{2,1,0:T(8,128)(2,1)S(1)} %broadcast_select_fusion.mid) | copy-start | bytes 2359300
  3.7 4.5 %copy-start.5 = (f32[3,16]{1,0:T(4,128)S(1)}, f32[3,16]{1,0:T(4,128)}, u32[]{:S(2)}) copy-start(f32[3,16]{1,0:T(4,128)} %param.13) | copy-start | bytes 580
  3.7 5.9 %collective-permute-start.1 = (bf16[2,8,12288]{2,1,0:T(8,128)(2,1)S(1)}, bf16[2,8,12288]{2,1,0:T(8,128)(2,1)S(1)}, u32[]{:S(2)}, u32[]{:S(2)}) collective-permute-start(bf16[2,8,12288]{2,1,0:T(8,128)(2,1)S(1)} %get-tuple-element.3), channel_id=1, source_target_pairs={{1,0},{2,1},{3,2},{4,3},{5,4},{6,5},{7,6},{8,7},{9,8},{10,9},{11,1... | collective-permute-start | bytes 1179656 | tf_op jit(solution)/shard_map/ppermute | solution.py:200
  5.2 4.5 %collective-permute-start = (bf16[2,8,12288]{2,1,0:T(8,128)(2,1)S(1)}, bf16[2,8,12288]{2,1,0:T(8,128)(2,1)S(1)}, u32[]{:S(2)}, u32[]{:S(2)}) collective-permute-start(bf16[2,8,12288]{2,1,0:T(8,128)(2,1)S(1)} %get-tuple-element.4), channel_id=1, source_target_pairs={{0,1},{1,2},{2,3},{3,4},{4,5},{5,6},{6,7},{7,8},{8,9},{9,10},{10,1... | collective-permute-start | bytes 1179656 | tf_op jit(solution)/shard_map/ppermute | solution.py:199
  8.2 0.7 copy-start.6
  9.6 0.8 %copy-start.1 = (bf16[2,8,12288]{2,1,0:T(8,128)(2,1)}, bf16[2,8,12288]{2,1,0:T(8,128)(2,1)S(1)}, u32[]{:S(2)}) copy-start(bf16[2,8,12288]{2,1,0:T(8,128)(2,1)S(1)} %collective-permute-done.1.high) | copy-start | bytes 1179652
  10.4 0.7 %copy-start.2 = (bf16[2,8,12288]{2,1,0:T(8,128)(2,1)}, bf16[2,8,12288]{2,1,0:T(8,128)(2,1)S(1)}, u32[]{:S(2)}) copy-start(bf16[2,8,12288]{2,1,0:T(8,128)(2,1)S(1)} %collective-permute-done.low) | copy-start | bytes 1179652

commit v2 on v1

v2 whole, which is shorter than its diff:
```python
import functools

import jax
import jax.numpy as jnp
from jax import lax
from jax.experimental import pallas as pl
from jax.experimental.pallas import tpu as pltpu
from jax.sharding import PartitionSpec as P

HALO = 8
TAPS = 11
NOTE = 8
STEP = 512
PI = 3.141592653589793
HALF = 0.7071067811865476
COS8 = (1.0, HALF, 0.0, -HALF, -1.0, -HALF, 0.0, HALF)


def range_weights(coef, start, weight, cols):
    for g in range(cols // 1024):
        centre = (g * 1024 + 512) / cols
        oc = coef[0] + coef[1] * centre + coef[2] * (centre * centre) + coef[3] * (centre**3)
        n0 = (oc - 5.0 + 64.0).astype(jnp.int32) - 63
        start[g] = n0
        sub = lax.broadcasted_iota(jnp.int32, (8, 128), 0)
        lane = lax.broadcasted_iota(jnp.int32, (8, 128), 1)
        col = g * 1024 + sub * 128 + lane
        v = (col.astype(jnp.float32) + 0.5) / cols
        off = coef[0] + coef[1] * v + coef[2] * v * v + coef[3] * v * v * v
        whole = jnp.round(off)
        part = off - whole
        odd = (whole.astype(jnp.int32) + n0) & 1
        sine = jnp.sin(PI * part) * (-1.0 / PI) * (1 - 2 * odd).astype(jnp.float32)
        base = (n0.astype(jnp.float32) - off) * (PI / 4.0)
        c0, s0 = jnp.cos(base), jnp.sin(base)
        for k in range(TAPS):
            n = n0 + k
            d = n.astype(jnp.float32) - off
            ck, sk = COS8[k % 8], COS8[(k - 2) % 8]
            taper = 0.5 + 0.5 * (c0 * ck - s0 * sk)
            top = sine if k % 2 == 0 else -sine
            near = d == 0.0
            val = jnp.where(near, 1.0, top / jnp.where(near, 1.0, d)) * taper
            keep = (jnp.abs(d) < 4.0) & (col + n >= 0) & (col + n < cols)
            val = jnp.where(keep, val, 0.0)
            weight[g, k] = val.astype(jnp.bfloat16).astype(jnp.float32)


def column(values):
    row = lax.broadcasted_iota(jnp.int32, (len(values), 128), 0)
    made = jnp.zeros((len(values), 128), jnp.asarray(values[0]).dtype)
    for r, value in enumerate(values):
        made = jnp.where(row == r, value, made)
    return made


def azimuth_band(fraction, base, line, blocks):
    held = lax.broadcasted_iota(jnp.int32, (blocks, 128), 1)
    row = jnp.where(held < blocks, held, held - blocks - HALO)
    row = jnp.where(held < blocks + HALO, row, held - HALO)
    gap = row - line - base
    d = gap.astype(jnp.float32) - fraction
    near = d == 0.0
    safe = jnp.where(near, 1.0, d)
    whole = jnp.round(safe)
    sine = jnp.sin(PI * (safe - whole)) * (1 - 2 * (whole.astype(jnp.int32) & 1)).astype(jnp.float32)
    value = jnp.where(near, 1.0, sine / (PI * safe)) * (0.5 + 0.5 * jnp.cos(PI * d / 4.0))
    keep = (jnp.abs(d) < 4.0) & (jnp.abs(gap) <= 4) & (held < blocks + 2 * HALO)
    return jnp.where(keep, value, 0.0).astype(jnp.bfloat16)


def swath_kernel(
    chunks, coef, shift, dest, valid, first, last, az_coef, az_base, image,
    got, notes,
    held, edge, dense, weight, sent, memo, start, order,
    own_sem, halo_send, halo_recv, edge_send, edge_recv, send_sem, recv_sem, note_send, note_recv,
):
    blocks, cols = image.shape[1], image.shape[2]
    tiles = cols // 128
    span = dense.shape[0] // (2 * blocks)
    count = lax.axis_size("az")
    me = lax.axis_index("az")
    after, before = lax.rem(me + 1, count), lax.rem(me + count - 1, count)
    own = pltpu.make_async_copy(image, held.at[:, pl.ds(0, blocks)], own_sem)
    own.start()

    barrier = pltpu.get_barrier_semaphore()

    def greet(i, carry):
        pl.semaphore_signal(barrier, inc=1, device_id={"az": lax.rem(me + 1 + i, count)})
        return carry

    lax.fori_loop(0, count - 1, greet, 0)
    low_edge = [jnp.where(valid[r] > 0, first[r], cols) for r in range(blocks)]
    high_edge = [jnp.where(valid[r] > 0, last[r], 0) for r in range(blocks)]
    edge[0, pl.ds(0, blocks), :] = column(low_edge).astype(jnp.float32)
    edge[1, pl.ds(0, blocks), :] = column(high_edge).astype(jnp.float32)
    pl.semaphore_wait(barrier, count - 1)

    steps = cols // STEP
    bounds = [0] + [steps * (c + 1) // chunks + 1 for c in range(chunks - 1)] + [steps]
    ways = ((after, blocks - HALO, blocks), (before, 0, blocks + HALO))
    for w, (peer, source, slot) in enumerate(ways):
        pltpu.make_async_remote_copy(
            src_ref=edge.at[:, pl.ds(source, HALO), :],
            dst_ref=edge.at[:, pl.ds(slot, HALO), :],
            send_sem=edge_send.at[w],
            recv_sem=edge_recv.at[w],
            device_id={"az": peer},
        ).start()
    halo = []
    for c in range(chunks):
        at = pl.ds(bounds[c] * STEP, (bounds[c + 1] - bounds[c]) * STEP)
        for w, (peer, source, slot) in enumerate(ways):
            copy = pltpu.make_async_remote_copy(
                src_ref=image.at[:, pl.ds(source, HALO), at],
                dst_ref=held.at[:, pl.ds(slot, HALO), at],
                send_sem=halo_send.at[c, w],
                recv_sem=halo_recv.at[c, w],
                device_id={"az": peer},
            )
            copy.start()
            halo.append(copy)

    range_weights(coef, start, weight, cols)
    lines = []
    for i in range(blocks):
        target = lax.rem(me + 1 + i, count)
        line = jnp.int32(0)
        for j in range(blocks):
            line = jnp.where(dest[j] // blocks == target, j, line)
        order[i] = line
        lines.append(line)
    c0 = column([az_coef[0, j] for j in lines])
    c1 = column([az_coef[1, j] for j in lines])
    c2 = column([az_coef[2, j] for j in lines])
    q = 0.5
    fraction = c0 + c1 * q + c2 * q * q
    band = azimuth_band(fraction, column([az_base[j] for j in lines]), column(lines), blocks)
    band = band[:, : blocks + 2 * HALO]

    own.wait()
    for w, (peer, source, slot) in enumerate(ways):
        pltpu.make_async_remote_copy(
            src_ref=edge.at[:, pl.ds(source, HALO), :],
            dst_ref=edge.at[:, pl.ds(slot, HALO), :],
            send_sem=edge_send.at[w],
            recv_sem=edge_recv.at[w],
            device_id={"az": peer},
        ).wait()
    low = edge[0]
    high = edge[1]
    row = lax.broadcasted_iota(jnp.int32, high.shape, 0)
    outside = ((me == 0) & (row >= blocks) & (row < blocks + HALO)) | (
        (me == count - 1) & (row >= blocks + HALO)
    )
    high = jnp.where(outside, 0.0, high)
    lane_held = lax.broadcasted_iota(jnp.int32, high.shape, 1).astype(jnp.float32)
    lane_row = lax.broadcasted_iota(jnp.int32, (blocks, 128), 1)
    lane = lax.broadcasted_iota(jnp.int32, (8, 128), 1)

    def azimuth(s, tails):
        at = pl.ds(pl.multiple_of(s * STEP, STEP), STEP)
        keeps = []
        for u in range(STEP // 128):
            col = lane_held + (s * STEP + u * 128).astype(jnp.float32)
            keeps.append((col >= low) & (col < high))
        new_tails = []
        for p in range(2):
            rows = held[p, :, at].astype(jnp.float32)
            rows = jnp.concatenate(
                [
                    jnp.where(keep, rows[:, u * 128 : u * 128 + 128], 0.0)
                    for u, keep in enumerate(keeps)
                ],
                axis=1,
            ).astype(jnp.bfloat16)
            out = jnp.dot(band, rows, preferred_element_type=jnp.float32)
            out = out.astype(jnp.bfloat16).astype(jnp.float32)
            tail = tails[p]
            for u in range(STEP // 128):
                turned = pltpu.roll(out[:, u * 128 : u * 128 + 128], 64, 1)
                place = p * blocks * span + s * (STEP // 128) + u
                dense[pl.ds(place, blocks, stride=span), :] = jnp.where(lane_row < 64, tail, turned)
                tail = turned
            new_tails.append(tail)
        return tuple(new_tails)

    def filtered(i, big, power):
        for p in range(2):
            halves = []
            for h in range(2):
                g = big * 2 + h
                b = shift[order[i]] + start[g] + 64
                at = pl.multiple_of((p * blocks + i) * span + g * 8, 8)
                x0 = dense[pl.ds(at, 8), :]
                x1 = dense[pl.ds(at + 1, 8), :]
                acc = None
                for k in range(TAPS):
                    moved = pltpu.roll(jnp.where(lane < b + k, x1, x0), 128 - b - k, 1)
                    term = weight[g, k] * moved
                    acc = term if acc is None else acc + term
                halves.append(acc)
            done = jnp.concatenate(halves, axis=0).astype(jnp.bfloat16)
            sent[i, p, pl.ds(pl.multiple_of(big * 16, 16), 16), :] = done
            wide = done.astype(jnp.float32)
            power = power + wide * wide
        return power

    tails = (jnp.zeros((blocks, 128), jnp.float32),) * 2
    power = jnp.zeros((16, 128), jnp.float32)
    bigs = tiles // 16
    for c in range(chunks):
        for copy in halo[2 * c : 2 * c + 2]:
            copy.wait()
        tails = lax.fori_loop(bounds[c], bounds[c + 1], azimuth, tails)
        if c == chunks - 1:
            for p in range(2):
                ends = jnp.where(lane_row < 64, tails[p], 0.0)
                dense[pl.ds(p * blocks * span + tiles, blocks, stride=span), :] = ends
        lo, hi = bigs * c // chunks, bigs * (c + 1) // chunks
        at = pl.ds(lo * 16, (hi - lo) * 16)

        def line(i, power):
            power = lax.fori_loop(lo, hi, functools.partial(filtered, i), power, unroll=True)

            @pl.when(i < count - 1)
            def _():
                pltpu.make_async_remote_copy(
                    src_ref=sent.at[i, :, at, :],
                    dst_ref=got.at[me, :, at, :],
                    send_sem=send_sem.at[c, i],
                    recv_sem=recv_sem.at[c, me],
                    device_id={"az": lax.rem(me + 1 + i, count)},
                ).start()

            return power

        power = lax.fori_loop(0, blocks, line, power)

    own_power = jnp.broadcast_to(jnp.sum(power, keepdims=True), (NOTE, 128))
    have = jnp.int32(0)
    for j in range(blocks):
        have = have + jnp.maximum(
            jnp.minimum(high_edge[j], cols) - jnp.maximum(low_edge[j], 0), 0
        )
    own_count = jnp.full((NOTE, 128), have, jnp.int32).astype(jnp.float32)
    row = lax.broadcasted_iota(jnp.int32, (NOTE, 128), 0)
    stats = jnp.where(row == 1, own_power, own_count)
    for i in range(blocks):
        place = jnp.full((NOTE, 128), dest[lines[i]] % blocks, jnp.int32).astype(jnp.float32)
        memo[i] = jnp.where(row == 0, place, stats)

    def tell(i, carry):
        pltpu.make_async_remote_copy(
            src_ref=memo.at[i],
            dst_ref=notes.at[me],
            send_sem=note_send.at[i],
            recv_sem=note_recv.at[me],
            device_id={"az": lax.rem(me + 1 + i, count)},
        ).start()
        return carry

    lax.fori_loop(0, count - 1, tell, 0)
    notes[me] = memo[blocks - 1]
    got[me] = sent[blocks - 1]

    def take(i, carry):
        peer = lax.rem(me + 1 + i, count)
        for c in range(chunks):
            lo, hi = bigs * c // chunks, bigs * (c + 1) // chunks
            at = pl.ds(lo * 16, (hi - lo) * 16)
            done = pltpu.make_async_remote_copy(
                src_ref=sent.at[i, :, at, :],
                dst_ref=got.at[peer, :, at, :],
                send_sem=send_sem.at[c, i],
                recv_sem=recv_sem.at[c, peer],
                device_id={"az": peer},
            )
            done.wait_send()
            done.wait_recv()
        told = pltpu.make_async_remote_copy(
            src_ref=memo.at[i],
            dst_ref=notes.at[peer],
            send_sem=note_send.at[i],
            recv_sem=note_recv.at[peer],
            device_id={"az": peer},
        )
        told.wait_send()
        told.wait_recv()
        return carry

    lax.fori_loop(0, count - 1, take, 0)


def finish_kernel(total, got, notes, out, mean, share, wide):
    blocks, cols = out.shape[1], out.shape[2]
    tiles = cols // 128
    told = [notes[s] for s in range(blocks)]
    both = functools.reduce(lambda a, b: a + b, told)
    power, count = both[1:2], both[2:3]
    mean_power = power / jnp.maximum(count, 1.0)
    gain = lax.rsqrt(mean_power + 0.5)
    mean[0] = mean_power[0, 0]
    share[0] = (count / float(total))[0, 0]
    for s in range(blocks):
        place = told[s][0, 0].astype(jnp.int32)
        for p in range(2):
            x = got[s, p].astype(jnp.float32) * gain
            wide[pl.ds(pl.multiple_of((p * blocks + place) * tiles, 8), tiles), :] = x

    def tile(t, carry):
        at = pl.ds(pl.multiple_of(t * 128, 128), 128)
        for p in range(2):
            x = wide[pl.ds(p * blocks * tiles + t, blocks, stride=tiles), :]
            out[p, :, at] = x.astype(jnp.bfloat16)
        return carry

    lax.fori_loop(0, tiles, tile, 0, unroll=8)


def shards(
    secondary, line_valid, first_valid, last_valid, az_coef, az_base, rg_base, rg_coef, block_dest
):
    cols = secondary.shape[2]
    blocks = block_dest.shape[0]
    tiles = cols // 128
    count = lax.axis_size("az")
    bigs = tiles // 16
    chunks = max(c for c in range(1, CHUNKS + 1) if bigs % c == 0)
    smem = pl.BlockSpec(memory_space=pltpu.SMEM)
    vmem = pl.BlockSpec(memory_space=pltpu.VMEM)
    held = blocks + 2 * HALO
    dma = pltpu.SemaphoreType.DMA
    got, notes = pl.pallas_call(
        functools.partial(swath_kernel, chunks),
        out_shape=(
            jax.ShapeDtypeStruct((blocks, 2, tiles, 128), jnp.bfloat16),
            jax.ShapeDtypeStruct((blocks, NOTE, 128), jnp.float32),
        ),
        in_specs=[smem] * 8 + [pl.BlockSpec(memory_space=pl.ANY)],
        out_specs=(vmem, vmem),
        scratch_shapes=[
            pltpu.VMEM((2, held, cols), jnp.bfloat16),
            pltpu.VMEM((2, held, 128), jnp.float32),
            pltpu.VMEM((2 * blocks * (tiles + 8), 128), jnp.float32),
            pltpu.VMEM((tiles // 8, TAPS, 8, 128), jnp.float32),
            pltpu.VMEM((blocks, 2, tiles, 128), jnp.bfloat16),
            pltpu.VMEM((blocks, NOTE, 128), jnp.float32),
            pltpu.SMEM((tiles // 8,), jnp.int32),
            pltpu.SMEM((blocks,), jnp.int32),
            dma(()),
            dma((chunks, 2)),
            dma((chunks, 2)),
            dma((2,)),
            dma((2,)),
            dma((chunks, blocks)),
            dma((chunks, blocks)),
            dma((blocks,)),
            dma((blocks,)),
        ],
        compiler_params=pltpu.CompilerParams(collective_id=0, has_side_effects=True),
        name="swath",
    )(
        rg_coef, rg_base, block_dest, line_valid, first_valid, last_valid, az_coef, az_base,
        secondary,
    )
    return pl.pallas_call(
        functools.partial(finish_kernel, cols * blocks * count),
        out_shape=(
            jax.ShapeDtypeStruct((2, blocks, cols), jnp.bfloat16),
            jax.ShapeDtypeStruct((1,), jnp.float32),
            jax.ShapeDtypeStruct((1,), jnp.float32),
        ),
        in_specs=[vmem, vmem],
        out_specs=(vmem, smem, smem),
        scratch_shapes=[pltpu.VMEM((2 * blocks * tiles, 128), jnp.float32)],
        name="finish",
    )(got, notes)


CHUNKS = 3


def solution(mesh):
    rows = P(("scene", "az"))
    placed = (
        P(None, ("scene", "az"), None),
        rows,
        rows,
        rows,
        P(None, ("scene", "az")),
        rows,
        rows,
        P("scene"),
        rows,
    )
    return jax.shard_map(
        shards,
        mesh=mesh,
        in_specs=placed,
        out_specs=(P(None, ("scene", "az"), None), P("scene"), P("scene")),
        check_vma=False,
    )
```

time: 71.8 us -> 41 us (0.57); the launches traced: 70.9 us -> 40.8 us
  blocking collectives: 35.5 us -> 0 us
  Pallas kernels: 24.3 us -> 40.2 us
  starting transfers between devices: 4.47 us -> 0 us
  local copies, waits for them, and re-layouts: 3.03 us -> 0 us
  other arithmetic: 2.91 us -> 0 us
    all_to_all x1 -> x0, blocking collectives: 35.5 us -> none  [shards(): got = lax.all_to_all(sent, 'az', split_axis=0, concat_axis=0, tiled=True)]
    pallas_call x1, Pallas kernels: 21 us -> 36.9 us  [shards(): pl.pallas_call(functools.partial(swath_kernel, chunks), out_shape=(jax.Sh...]
    ppermute x2 -> x0, starting transfers between devices: 4.47 us -> none  [the longest x1 3.05 us: shards(): low = lax.ppermute(masked[:, blocks - HALO:], 'az', forward)]
    unnamed x14 -> x0, local copies, waits for them, and re-layouts: 2.97 us -> none
    select_n x2 -> x0, other arithmetic: 1.24 us -> none  [the longest x1 1.23 us: shards(): masked = jnp.where(kept[None], secondary, jnp.zeros((), jnp.bfloat16))]
    convert_element_type x1 -> x0, other arithmetic: 0.72 us -> none  [azimuth_band(): return jnp.where(jnp.abs(gap) <= 4, value, 0.0).astype(jnp.bfloat16)]
  transfers between devices with their start and end apart: 2 -> 0, of which waited for: 0 -> 0; matrix products, arithmetic and copies ran while one was open for 1% -> 0% of each run, Pallas kernels for 0% -> 0%
where the time goes in v2:
time: 41 us; the launch traced here: 40.8 us
  Pallas kernels  40.2 us (98%)
  between operations  0.64 us (2%)
    pallas_call x1, Pallas kernels, shards(): pl.pallas_call(functools.partial(swath_kernel, chunks), out_shape=(jax.Sh...  36.9 us
    pallas_call x1, Pallas kernels, shards(): pl.pallas_call(functools.partial(finish_kernel, cols * blocks * count), o...  3.29 us

profile of v2, /device:TPU:0, one launch (start us, length us, event | category | flops | bytes accessed | tf_op | source)
XLA Modules:
  0.0 40.8 jit_solution(2513965913026525794)
XLA Ops:
  0.6 36.9 %swath.1 = (bf16[16,2,96,128]{3,2,1,0:T(8,128)(2,1)}, f32[16,8,128]{2,1,0:T(8,128)}) custom-call(f32[4]{0:T(128)} %coef.1, s32[16]{0:T(128)} %shift.1, s32[16]{0:T(128)} %dest.1, s32[16]{0:T(128)} %valid.1, s32[16]{0:T(128)} %first.1, s32[16]{0:T(128)} %last.1, f32[3,16]{1,0:T(4,128)} %az_coef.1, s32[16]{0:T(128)} %az_base.1, bf16[2,16,12288]{2,1,0:T(8,128)(2,1)} %image.1), custom_call_target="tpu_custom_call" | custom-call | tf_op jit(solution)/shard_map/swath/pallas_call | solution.py:335
  37.5 3.3 %finish.1 = (bf16[2,16,12288]{2,1,0:T(8,128)(2,1)}, f32[1]{0:T(128)}, f32[1]{0:T(128)}) custom-call(bf16[16,2,96,128]{3,2,1,0:T(8,128)(2,1)} %get-tuple-element.5.got, f32[16,8,128]{2,1,0:T(8,128)} %get-tuple-element.6.notes), custom_call_target="tpu_custom_call" | custom-call | tf_op jit(solution)/shard_map/finish/pallas_call | solution.py:368

commit v3 on v2

--- a/solution.py
+++ b/solution.py
@@ -69,8 +69,16 @@
     return jnp.where(keep, value, 0.0).astype(jnp.bfloat16)
 
 
+def send_order(me, count, i):
+    half = count // 2
+    mine = me // half
+    own = i // half
+    side = mine * own + (1 - mine) * (1 - own)
+    return side * half + lax.rem(me - mine * half + own + i - own * half, half)
+
+
 def swath_kernel(
-    chunks, coef, shift, dest, valid, first, last, az_coef, az_base, image,
+    cuts, coef, shift, dest, valid, first, last, az_coef, az_base, image,
     got, notes,
     held, edge, dense, weight, sent, memo, start, order,
     own_sem, halo_send, halo_recv, edge_send, edge_recv, send_sem, recv_sem, note_send, note_recv,
@@ -95,10 +103,29 @@
     high_edge = [jnp.where(valid[r] > 0, last[r], 0) for r in range(blocks)]
     edge[0, pl.ds(0, blocks), :] = column(low_edge).astype(jnp.float32)
     edge[1, pl.ds(0, blocks), :] = column(high_edge).astype(jnp.float32)
+    range_weights(coef, start, weight, cols)
+    lines = []
+    for i in range(blocks):
+        target = send_order(me, count, i)
+        line = jnp.int32(0)
+        for j in range(blocks):
+            line = jnp.where(dest[j] // blocks == target, j, line)
+        order[i] = line
+        lines.append(line)
+    c0 = column([az_coef[0, j] for j in lines])
+    c1 = column([az_coef[1, j] for j in lines])
+    c2 = column([az_coef[2, j] for j in lines])
+    q = 0.5
+    fraction = c0 + c1 * q + c2 * q * q
+    band = azimuth_band(fraction, column([az_base[j] for j in lines]), column(lines), blocks)
+    band = band[:, : blocks + 2 * HALO]
+
     pl.semaphore_wait(barrier, count - 1)
 
     steps = cols // STEP
-    bounds = [0] + [steps * (c + 1) // chunks + 1 for c in range(chunks - 1)] + [steps]
+    chunks = len(cuts) - 1
+    per = steps // (tiles // 16)
+    bounds = [0] + [cut * per + 1 for cut in cuts[1:-1]] + [steps]
     ways = ((after, blocks - HALO, blocks), (before, 0, blocks + HALO))
     for w, (peer, source, slot) in enumerate(ways):
         pltpu.make_async_remote_copy(
@@ -121,23 +148,6 @@
             )
             copy.start()
             halo.append(copy)
-
-    range_weights(coef, start, weight, cols)
-    lines = []
-    for i in range(blocks):
-        target = lax.rem(me + 1 + i, count)
-        line = jnp.int32(0)
-        for j in range(blocks):
-            line = jnp.where(dest[j] // blocks == target, j, line)
-        order[i] = line
-        lines.append(line)
-    c0 = column([az_coef[0, j] for j in lines])
-    c1 = column([az_coef[1, j] for j in lines])
-    c2 = column([az_coef[2, j] for j in lines])
-    q = 0.5
-    fraction = c0 + c1 * q + c2 * q * q
-    band = azimuth_band(fraction, column([az_base[j] for j in lines]), column(lines), blocks)
-    band = band[:, : blocks + 2 * HALO]
 
     own.wait()
     for w, (peer, source, slot) in enumerate(ways):
@@ -209,7 +219,6 @@
 
     tails = (jnp.zeros((blocks, 128), jnp.float32),) * 2
     power = jnp.zeros((16, 128), jnp.float32)
-    bigs = tiles // 16
     for c in range(chunks):
         for copy in halo[2 * c : 2 * c + 2]:
             copy.wait()
@@ -218,7 +227,7 @@
             for p in range(2):
                 ends = jnp.where(lane_row < 64, tails[p], 0.0)
                 dense[pl.ds(p * blocks * span + tiles, blocks, stride=span), :] = ends
-        lo, hi = bigs * c // chunks, bigs * (c + 1) // chunks
+        lo, hi = cuts[c], cuts[c + 1]
         at = pl.ds(lo * 16, (hi - lo) * 16)
 
         def line(i, power):
@@ -231,7 +240,7 @@
                     dst_ref=got.at[me, :, at, :],
                     send_sem=send_sem.at[c, i],
                     recv_sem=recv_sem.at[c, me],
-                    device_id={"az": lax.rem(me + 1 + i, count)},
+                    device_id={"az": send_order(me, count, i)},
                 ).start()
 
             return power
@@ -257,7 +266,7 @@
             dst_ref=notes.at[me],
             send_sem=note_send.at[i],
             recv_sem=note_recv.at[me],
-            device_id={"az": lax.rem(me + 1 + i, count)},
+            device_id={"az": send_order(me, count, i)},
         ).start()
         return carry
 
@@ -266,9 +275,9 @@
     got[me] = sent[blocks - 1]
 
     def take(i, carry):
-        peer = lax.rem(me + 1 + i, count)
+        peer = send_order(me, count, i)
         for c in range(chunks):
-            lo, hi = bigs * c // chunks, bigs * (c + 1) // chunks
+            lo, hi = cuts[c], cuts[c + 1]
             at = pl.ds(lo * 16, (hi - lo) * 16)
             done = pltpu.make_async_remote_copy(
                 src_ref=sent.at[i, :, at, :],
@@ -308,15 +317,10 @@
         for p in range(2):
             x = got[s, p].astype(jnp.float32) * gain
             wide[pl.ds(pl.multiple_of((p * blocks + place) * tiles, 8), tiles), :] = x
-
-    def tile(t, carry):
-        at = pl.ds(pl.multiple_of(t * 128, 128), 128)
+    for t in range(tiles):
         for p in range(2):
             x = wide[pl.ds(p * blocks * tiles + t, blocks, stride=tiles), :]
-            out[p, :, at] = x.astype(jnp.bfloat16)
-        return carry
-
-    lax.fori_loop(0, tiles, tile, 0, unroll=8)
+            out[p, :, t * 128 : t * 128 + 128] = x.astype(jnp.bfloat16)
 
 
 def shards(
@@ -327,13 +331,15 @@
     tiles = cols // 128
     count = lax.axis_size("az")
     bigs = tiles // 16
-    chunks = max(c for c in range(1, CHUNKS + 1) if bigs % c == 0)
+    cuts = [0] + sorted({bigs * cut // 6 for cut in CUTS} - {0, bigs}) + [bigs]
+    chunks = len(cuts) - 1
+    parts = max(c for c in range(1, PARTS + 1) if bigs % c == 0)
     smem = pl.BlockSpec(memory_space=pltpu.SMEM)
     vmem = pl.BlockSpec(memory_space=pltpu.VMEM)
     held = blocks + 2 * HALO
     dma = pltpu.SemaphoreType.DMA
     got, notes = pl.pallas_call(
-        functools.partial(swath_kernel, chunks),
+        functools.partial(swath_kernel, cuts),
         out_shape=(
             jax.ShapeDtypeStruct((blocks, 2, tiles, 128), jnp.bfloat16),
             jax.ShapeDtypeStruct((blocks, NOTE, 128), jnp.float32),
@@ -372,14 +378,16 @@
             jax.ShapeDtypeStruct((1,), jnp.float32),
             jax.ShapeDtypeStruct((1,), jnp.float32),
         ),
-        in_specs=[vmem, vmem],
-        out_specs=(vmem, smem, smem),
-        scratch_shapes=[pltpu.VMEM((2 * blocks * tiles, 128), jnp.float32)],
+        grid=(parts,),
+        in_specs=[pl.BlockSpec((blocks, 2, tiles // parts, 128), lambda c: (0, 0, c, 0)), vmem],
+        out_specs=(pl.BlockSpec((2, blocks, cols // parts), lambda c: (0, 0, c)), smem, smem),
+        scratch_shapes=[pltpu.VMEM((2 * blocks * (tiles // parts), 128), jnp.float32)],
         name="finish",
     )(got, notes)
 
 
-CHUNKS = 3
+CUTS = (2,)
+PARTS = 2
 
 
 def solution(mesh):

time: 41 us -> 40.2 us (0.980)
  Pallas kernels: 40.2 us -> 39.4 us
    pallas_call x1, Pallas kernels: 3.29 us -> 2.55 us  [shards(): pl.pallas_call(functools.partial(finish_kernel, cols * blocks * count), o...]
where the time goes in v3:
time: 40.2 us; the launch traced here: 40 us
  Pallas kernels  39.4 us (98%)
  between operations  0.64 us (2%)
    pallas_call x1, Pallas kernels, shards(): pl.pallas_call(functools.partial(swath_kernel, cuts), out_shape=(jax.Shap...  36.8 us
    pallas_call x1, Pallas kernels, shards(): pl.pallas_call(functools.partial(finish_kernel, cols * blocks * count), o...  2.55 us

profile of v3, /device:TPU:0, one launch (start us, length us, event | category | flops | bytes accessed | tf_op | source)
XLA Modules:
  0.0 40.0 jit_solution(348293872588812502)
XLA Ops:
  0.6 36.8 %swath.1 = (bf16[16,2,96,128]{3,2,1,0:T(8,128)(2,1)}, f32[16,8,128]{2,1,0:T(8,128)}) custom-call(f32[4]{0:T(128)} %coef.1, s32[16]{0:T(128)} %shift.1, s32[16]{0:T(128)} %dest.1, s32[16]{0:T(128)} %valid.1, s32[16]{0:T(128)} %first.1, s32[16]{0:T(128)} %last.1, f32[3,16]{1,0:T(4,128)} %az_coef.1, s32[16]{0:T(128)} %az_base.1, bf16[2,16,12288]{2,1,0:T(8,128)(2,1)} %image.1), custom_call_target="tpu_custom_call" | custom-call | tf_op jit(solution)/shard_map/swath/pallas_call | solution.py:341
  37.4 2.5 %finish.1 = (bf16[2,16,12288]{2,1,0:T(8,128)(2,1)}, f32[1]{0:T(128)}, f32[1]{0:T(128)}) custom-call(bf16[16,2,96,128]{3,2,1,0:T(8,128)(2,1)} %get-tuple-element.5.got, f32[16,8,128]{2,1,0:T(8,128)} %get-tuple-element.6.notes), custom_call_target="tpu_custom_call" | custom-call | tf_op jit(solution)/shard_map/finish/pallas_call | solution.py:374

commit v4 on v3

--- a/solution.py
+++ b/solution.py
@@ -81,7 +81,7 @@
     cuts, coef, shift, dest, valid, first, last, az_coef, az_base, image,
     got, notes,
     held, edge, dense, weight, sent, memo, start, order,
-    own_sem, halo_send, halo_recv, edge_send, edge_recv, send_sem, recv_sem, note_send, note_recv,
+    ready, own_sem, halo_send, halo_recv, edge_send, edge_recv, send_sem, recv_sem, note_send, note_recv,
 ):
     blocks, cols = image.shape[1], image.shape[2]
     tiles = cols // 128
@@ -94,33 +94,13 @@
 
     barrier = pltpu.get_barrier_semaphore()
 
-    def greet(i, carry):
-        pl.semaphore_signal(barrier, inc=1, device_id={"az": lax.rem(me + 1 + i, count)})
-        return carry
-
-    lax.fori_loop(0, count - 1, greet, 0)
+    for peer in (after, before):
+        pl.semaphore_signal(barrier, inc=1, device_id={"az": peer})
     low_edge = [jnp.where(valid[r] > 0, first[r], cols) for r in range(blocks)]
     high_edge = [jnp.where(valid[r] > 0, last[r], 0) for r in range(blocks)]
     edge[0, pl.ds(0, blocks), :] = column(low_edge).astype(jnp.float32)
     edge[1, pl.ds(0, blocks), :] = column(high_edge).astype(jnp.float32)
-    range_weights(coef, start, weight, cols)
-    lines = []
-    for i in range(blocks):
-        target = send_order(me, count, i)
-        line = jnp.int32(0)
-        for j in range(blocks):
-            line = jnp.where(dest[j] // blocks == target, j, line)
-        order[i] = line
-        lines.append(line)
-    c0 = column([az_coef[0, j] for j in lines])
-    c1 = column([az_coef[1, j] for j in lines])
-    c2 = column([az_coef[2, j] for j in lines])
-    q = 0.5
-    fraction = c0 + c1 * q + c2 * q * q
-    band = azimuth_band(fraction, column([az_base[j] for j in lines]), column(lines), blocks)
-    band = band[:, : blocks + 2 * HALO]
-
-    pl.semaphore_wait(barrier, count - 1)
+    pl.semaphore_wait(barrier, 2)
 
     steps = cols // STEP
     chunks = len(cuts) - 1
@@ -148,6 +128,36 @@
             )
             copy.start()
             halo.append(copy)
+
+    def meet(r):
+        for peer in (lax.rem(me + (1 << r), count), lax.rem(me + count - (1 << r), count)):
+            pl.semaphore_signal(ready.at[r], inc=1, device_id={"az": peer})
+
+    meetings = ready.shape[0]
+    meet(0)
+    lines = []
+    for i in range(blocks):
+        target = send_order(me, count, i)
+        line = jnp.int32(0)
+        for j in range(blocks):
+            line = jnp.where(dest[j] // blocks == target, j, line)
+        order[i] = line
+        lines.append(line)
+    c0 = column([az_coef[0, j] for j in lines])
+    c1 = column([az_coef[1, j] for j in lines])
+    c2 = column([az_coef[2, j] for j in lines])
+    q = 0.5
+    fraction = c0 + c1 * q + c2 * q * q
+    band = azimuth_band(fraction, column([az_base[j] for j in lines]), column(lines), blocks)
+    band = band[:, : blocks + 2 * HALO]
+    pl.semaphore_wait(ready.at[0], 2)
+    if meetings > 1:
+        meet(1)
+    range_weights(coef, start, weight, cols)
+    for r in range(1, meetings):
+        pl.semaphore_wait(ready.at[r], 2)
+        if r + 1 < meetings:
+            meet(r + 1)
 
     own.wait()
     for w, (peer, source, slot) in enumerate(ways):
@@ -355,6 +365,7 @@
             pltpu.VMEM((blocks, NOTE, 128), jnp.float32),
             pltpu.SMEM((tiles // 8,), jnp.int32),
             pltpu.SMEM((blocks,), jnp.int32),
+            pltpu.SemaphoreType.REGULAR((max(1, (count // 2 - 1).bit_length()),)),
             dma(()),
             dma((chunks, 2)),
             dma((chunks, 2)),

time: 40.2 us -> 39.6 us (0.985)
  Pallas kernels: 39.4 us -> 38.8 us
    pallas_call x1, Pallas kernels: 36.8 us -> 36.2 us  [shards(): pl.pallas_call(functools.partial(swath_kernel, cuts), out_shape=(jax.Shap...]
where the time goes in v4:
time: 39.6 us; the launch traced here: 39.4 us
  Pallas kernels  38.8 us (98%)
  between operations  0.64 us (2%)
    pallas_call x1, Pallas kernels, shards(): pl.pallas_call(functools.partial(swath_kernel, cuts), out_shape=(jax.Shap...  36.2 us
    pallas_call x1, Pallas kernels, shards(): pl.pallas_call(functools.partial(finish_kernel, cols * blocks * count), o...  2.55 us

profile of v4, /device:TPU:0, one launch (start us, length us, event | category | flops | bytes accessed | tf_op | source)
XLA Modules:
  0.0 39.4 jit_solution(5014366095657084133)
XLA Ops:
  0.6 36.2 %swath.1 = (bf16[16,2,96,128]{3,2,1,0:T(8,128)(2,1)}, f32[16,8,128]{2,1,0:T(8,128)}) custom-call(f32[4]{0:T(128)} %coef.1, s32[16]{0:T(128)} %shift.1, s32[16]{0:T(128)} %dest.1, s32[16]{0:T(128)} %valid.1, s32[16]{0:T(128)} %first.1, s32[16]{0:T(128)} %last.1, f32[3,16]{1,0:T(4,128)} %az_coef.1, s32[16]{0:T(128)} %az_base.1, bf16[2,16,12288]{2,1,0:T(8,128)(2,1)} %image.1), custom_call_target="tpu_custom_call" | custom-call | tf_op jit(solution)/shard_map/swath/pallas_call | solution.py:351
  36.8 2.6 %finish.1 = (bf16[2,16,12288]{2,1,0:T(8,128)(2,1)}, f32[1]{0:T(128)}, f32[1]{0:T(128)}) custom-call(bf16[16,2,96,128]{3,2,1,0:T(8,128)(2,1)} %get-tuple-element.5.got, f32[16,8,128]{2,1,0:T(8,128)} %get-tuple-element.6.notes), custom_call_target="tpu_custom_call" | custom-call | tf_op jit(solution)/shard_map/finish/pallas_call | solution.py:385
